TPU v7x, 32 devices: a whole 2x2x4 slice. The times are simulated.
32 devices in a mesh: gx: 4 (over y, x), gy: 2 (over core), gz: 4 (over z).
Axes of the slice: x: 2, y: 2, z: 4, core: 2. Of those that a mesh axis runs over, the one named last changes fastest.
Arguments:
- params: float32 [12, 7168, 1536], P('gx', 'gy', 'gz'), may hold values from -100 to 100
- grads: bfloat16 [12, 7168, 1536], P('gx', 'gy', 'gz'), may hold values from -300 to 300
- row_state: float32 [12, 7168], P('gx', 'gy'), may hold values from 0.01 to 1
- col_state: float32 [12, 1536], P('gx', 'gz'), may hold values from 0.01 to 1
Outputs:
- new_params: float32 [12, 7168, 1536], P('gx', 'gy', 'gz')
- row_new: float32 [12, 7168], P('gx', 'gy')
- col_new: float32 [12, 1536], P('gx', 'gz')
- applied_step: float32 [12, 7168, 1536], P('gx', 'gy', 'gz')
- compute_copy: bfloat16 [12, 7168, 1536], P('gx', 'gy')
All inputs are finite; a program needn't handle non-finite values.
Results may differ from a plain program's by a relative error of at most 0.0004.
Values may be sent and summed in bfloat16 or wider, within the bound.
A program may use at most 192 MiB of HBM per device.

v0:
```python
import jax
import jax.numpy as jnp
from jax import lax
from jax.sharding import PartitionSpec as P

decay_rate = 0.842
tiny_term = 1e-30
step_share = 0.01
clip_limit = 1.0


def factor_stats(weights, gradient, row_old, col_old):
    grad_float = gradient.astype(jnp.float32)
    squares = grad_float * grad_float + tiny_term
    columns = gradient.shape[2] * lax.axis_size("gz")
    rows_all = gradient.shape[1] * lax.axis_size("gy")
    row_sum = lax.psum(jnp.sum(squares, axis=2), "gz")
    col_sum = lax.psum(jnp.sum(squares, axis=1), "gy")
    row_new = decay_rate * row_old + (1.0 - decay_rate) * (row_sum / columns)
    col_new = decay_rate * col_old + (1.0 - decay_rate) * (col_sum / rows_all)
    weight_sq = jnp.sum(weights * weights, axis=(1, 2))
    weight_total = lax.psum(weight_sq, ("gy", "gz"))
    row_total = lax.psum(jnp.sum(row_new, axis=1), "gy")
    row_norm = row_new / (row_total / rows_all)[:, None]
    update = grad_float * lax.rsqrt(row_norm[:, :, None] * col_new[:, None, :])
    update_sq = jnp.sum(update * update, axis=(1, 2))
    weight_scale = jnp.sqrt(weight_total / (rows_all * columns))
    return (update, update_sq, weight_scale, row_new, col_new)


def gather_copy(halves):
    return lax.all_gather(halves, "gz", axis=2, tiled=True)


def body(params, grads, row_state, col_state):
    update, update_sq, weight_scale, row_new, col_new = factor_stats(
        params, grads, row_state, col_state
    )
    update_total = lax.psum(jnp.sum(update_sq), ("gx", "gy", "gz"))
    entries = params.size * lax.axis_size("gx") * lax.axis_size("gy") * lax.axis_size("gz")
    root_mean = jnp.sqrt(update_total / entries)
    clip_factor = jnp.maximum(1.0, root_mean / clip_limit)
    applied = weight_scale[:, None, None] * update / clip_factor
    new_params = params - step_share * applied
    copy_half = new_params.astype(jnp.bfloat16)
    compute = gather_copy(copy_half)
    return (new_params, row_new, col_new, applied, compute)


def solution(mesh):
    in_specs = (P("gx", "gy", "gz"), P("gx", "gy", "gz"), P("gx", "gy"), P("gx", "gz"))
    out_specs = (
        P("gx", "gy", "gz"),
        P("gx", "gy"),
        P("gx", "gz"),
        P("gx", "gy", "gz"),
        P("gx", "gy", None),
    )
    return jax.shard_map(body, mesh=mesh, in_specs=in_specs, out_specs=out_specs, check_vma=False)
```

profile of v0, /device:TPU:0, one launch (start us, length us, event | category | flops | bytes accessed | tf_op | source)
XLA Modules:
  0.0 711.9 jit_solution(18052197399156086212)
XLA Ops:
  7.2 0.0 copy-start.1
  7.2 0.0 copy-start.3
  7.2 0.0 all-gather.2.cloned.1.call-start
  7.2 7.2 %multiply_reduce_fusion.1 = f32[3]{0:T(128)S(1)} fusion(f32[3,3584,384]{2,1,0:T(8,128)} %param.4), kind=kLoop, calls=%fused_computation.8 | loop fusion | flops 8257533 | bytes 16515084 | tf_op jit(solution)/shard_map/reduce_sum | solution.py:21
  14.5 18.5 %psum.35 = f32[3]{0:T(128)S(1)} all-reduce(f32[3]{0:T(128)S(1)} %multiply_reduce_fusion.1), channel_id=1, replica_groups=mesh['gx'=4,'gy'=2,'gz'=4] {'gy','gz'}, use_global_device_ids=true, to_apply=%region_1.0 | all-reduce | flops 3 | bytes 24 | tf_op jit(solution)/shard_map/psum | solution.py:22
  33.0 6.5 fusion.2
  39.4 16.8 %psum.36 = f32[3,3584]{1,0:T(4,128)S(1)} all-reduce(f32[3,3584]{1,0:T(4,128)S(1)} %get-tuple-element.5), channel_id=1, replica_groups=mesh['gx'=4,'gy'=2,'gz'=4] {'gz'}, use_global_device_ids=true, to_apply=%region_3.0 | all-reduce | flops 10752 | bytes 86016 | tf_op jit(solution)/shard_map/psum | solution.py:17
  56.3 0.0 copy-done.1
  56.3 0.1 fusion.4
  56.4 0.0 copy-start
  56.4 2.5 all-reduce
  58.9 0.0 copy-done.3
  59.0 0.0 copy-start.2
  59.0 0.1 broadcast_divide_fusion
  59.1 8.2 %multiply_reduce_fusion = f32[]{:T(128)} fusion(bf16[3,3584,384]{2,1,0:T(8,128)(2,1)} %param.5, f32[3,384]{1,0:T(4,128)S(1)} %multiply_add_fusion.1, f32[3,3584]{1,0:T(4,128)S(1)} %broadcast_divide_fusion), kind=kLoop, calls=%fused_computation.6 | loop fusion | flops 20643840 | bytes 8305156 | tf_op jit(solution)/shard_map/reduce_sum | solution.py:39
  67.3 38.7 %psum.39 = f32[]{:T(128)} all-reduce(f32[]{:T(128)} %multiply_reduce_fusion), channel_id=1, replica_groups=mesh['gx'=4,'gy'=2,'gz'=4] {'gx','gy','gz'}, use_global_device_ids=true, to_apply=%region_9.0 | all-reduce | flops 1 | bytes 8 | tf_op jit(solution)/shard_map/psum | solution.py:39
  106.7 22.5 %fusion.3 = (bf16[3,3584,384]{2,1,0:T(8,128)(2,1)}, f32[3,3584,384]{2,1,0:T(8,128)}, f32[3,3584,384]{2,1,0:T(8,128)}) fusion(f32[3,3584,384]{2,1,0:T(8,128)} %param.4, f32[]{:T(128)S(6)} %max.3, f32[3,384]{1,0:T(4,128)S(1)} %multiply_add_fusion.1, f32[3,3584]{1,0:T(4,128)S(1)} %broadcast_divide_fusion, bf16[3,3584,384]{2,1,0:T(8,128)(2,1)} %param.5, ...), kind=kLoop, calls=%fused_computation.14 | loop fusion | flops 33030144 | bytes 66107920 | tf_op jit(solution)/shard_map/convert_element_type | solution.py:45
  129.2 0.0 copy-done
  129.2 0.0 copy-done.2
  129.2 0.0 all-gather.2.cloned.1.call-update
  129.2 552.9 %all-gather.2.cloned.1.call-done = bf16[3,3584,1536]{2,1,0:T(8,128)(2,1)} async-done(((bf16[3,3584,384]{2,1,0:T(8,128)(2,1)}), bf16[3,3584,1536]{2,1,0:T(8,128)(2,1)}) %all-gather.2.cloned.1.call-update) | async-done | bytes 33030160 | tf_op jit(solution)/shard_map/all_gather | solution.py:32
  682.2 22.9 %copy.10 = bf16[3,3584,1536]{2,1,0:T(8,128)(2,1)} copy(bf16[3,3584,1536]{2,1,0:T(8,128)(2,1)} %all-gather.2.cloned.1.call-done) | data formatting | bytes 66060288
  (3 shorter events, 0.0 us)
Async XLA Ops:
  7.2 49.1 %copy-start.1 = (f32[3,3584]{1,0:T(4,128)S(1)}, f32[3,3584]{1,0:T(4,128)}, u32[]{:S(2)}) copy-start(f32[3,3584]{1,0:T(4,128)} %param.6) | copy-start | bytes 129028
  7.2 51.8 %copy-start.3 = (f32[3,384]{1,0:T(4,128)S(1)}, f32[3,384]{1,0:T(4,128)}, u32[]{:S(2)}) copy-start(f32[3,384]{1,0:T(4,128)} %param.7) | copy-start | bytes 13828
  7.2 675.0 %all-gather.2.cloned.1.call-start = ((), (), s32[]{:S(2)}) async-start(), calls=%async_computation | async-start | bytes 41287680 | tf_op jit(solution)/shard_map/all_gather | solution.py:32
  56.4 72.8 %copy-start = (f32[3,3584]{1,0:T(4,128)}, f32[3,3584]{1,0:T(4,128)S(1)}, u32[]{:S(2)}) copy-start(f32[3,3584]{1,0:T(4,128)S(1)} %get-tuple-element.20) | copy-start | bytes 129028
  59.0 70.2 %copy-start.2 = (f32[3,384]{1,0:T(4,128)}, f32[3,384]{1,0:T(4,128)S(1)}, u32[]{:S(2)}) copy-start(f32[3,384]{1,0:T(4,128)S(1)} %multiply_add_fusion.1) | copy-start | bytes 13828
Sparse Core Ops, SparseCore 0:
  129.3 552.7 all-gather.1
where the time goes:
time: 712 us
  waiting for transfers between devices  553 us (78%)
  blocking collectives  76.5 us (11%)
  other arithmetic  44.7 us (6%)
  local copies, waits for them, and re-layouts  22.9 us (3%)
  between operations  14.8 us (2%)
    all_gather x1, waiting for transfers between devices, gather_copy(): return lax.all_gather(halves, 'gz', axis=2, tiled=True)  553 us
    psum x1, blocking collectives, body(): update_total = lax.psum(jnp.sum(update_sq), ('gx', 'gy', 'gz'))  38.7 us
    unnamed x9, local copies, waits for them, and re-layouts  22.9 us
    convert_element_type x1, other arithmetic, body(): copy_half = new_params.astype(jnp.bfloat16)  22.5 us
    psum x1, blocking collectives, factor_stats(): weight_total = lax.psum(weight_sq, ('gy', 'gz'))  18.5 us
    psum x1, blocking collectives, factor_stats(): row_sum = lax.psum(jnp.sum(squares, axis=2), 'gz')  16.8 us
  transfers between devices with their start and end apart: 1, of which 1 were waited for; matrix products, arithmetic and copies ran while one was open for 0% of the time, Pallas kernels for 0%

commit v1 on v0

v1 whole, which is shorter than its diff:
```python
import functools
import jax
import jax.numpy as jnp
from jax import lax
from jax.experimental import pallas as pl
from jax.experimental.pallas import tpu as pltpu
from jax.sharding import PartitionSpec as P

decay_rate = 0.842
tiny_term = 1e-30
step_share = 0.01
clip_limit = 1.0
LANES = 128
f32, bf16 = jnp.float32, jnp.bfloat16


def fold(values):
    return jnp.sum(values.reshape(values.shape[0] // 8, 8, values.shape[1]), axis=0)


def fold_lanes(row):
    return sum(row[:, i : i + LANES] for i in range(0, row.shape[1], LANES))


def split(values):
    high = values.astype(bf16)
    return high, (values - high.astype(f32)).astype(bf16)


def row_dots(left, values):
    dims = (((1,), (1,)), ((), ()))
    high, low = split(values)
    return lax.dot_general(left, high, dims, preferred_element_type=f32) + lax.dot_general(
        left, low, dims, preferred_element_type=f32
    )


def exchange(axis, bufs, send, recv):
    n, me = lax.axis_size(axis), lax.axis_index(axis)
    copies = []
    for i, buf in enumerate(bufs):
        for d in range(1, n):
            slot = i * (n - 1) + d - 1
            copy = pltpu.make_async_remote_copy(
                src_ref=buf.at[me],
                dst_ref=buf.at[me],
                send_sem=send.at[slot],
                recv_sem=recv.at[slot],
                device_id={axis: lax.rem(me + d, n)},
                device_id_type=pl.DeviceIdType.MESH,
            )
            copy.start()
            copies.append(copy)
    return copies


def finish(copies):
    for copy in copies:
        copy.wait()


def total(buf):
    return functools.reduce(lambda a, b: a + b, [buf[i] for i in range(buf.shape[0])])


def stats_kernel(
    layers, chunk, small,
    p_hbm, g_hbm, row_ref, col_ref,
    row_out, col_out, rr_out, rc_out, big_hbm, small_hbm,
    p_vm, g_vm, new_vm, row_all, col_all, sc_z, sc_y, up_z, up_y, up_x,
    p_sem, g_sem, o_sem,
    rz_s, rz_r, cy_s, cy_r, sy_s, sy_r, uz_s, uz_r, uy_s, uy_r, ux_s, ux_r,
):
    rows_total, columns = g_vm.shape
    rows = rows_total // layers
    nb, per, chunks = rows // LANES, chunk // LANES, rows // chunk
    nx, ny, nz = (lax.axis_size(a) for a in ("gx", "gy", "gz"))
    me_x, me_y, me_z = (lax.axis_index(a) for a in ("gx", "gy", "gz"))
    rows_all, columns_all = rows * ny, columns * nz

    loads = []
    for k in range(layers * chunks):
        part = pl.ds(k * chunk, chunk)
        g_copy = pltpu.make_async_copy(g_hbm.at[part], g_vm.at[part], g_sem.at[k])
        p_copy = pltpu.make_async_copy(p_hbm.at[part], p_vm.at[part], p_sem.at[k])
        g_copy.start()
        p_copy.start()
        loads.append((g_copy, p_copy))

    barrier = pltpu.get_barrier_semaphore()
    for axis, n, me in (("gx", nx, me_x), ("gy", ny, me_y), ("gz", nz, me_z)):
        for d in range(1, n):
            pl.semaphore_signal(
                barrier, inc=1, device_id={axis: lax.rem(me + d, n)},
                device_id_type=pl.DeviceIdType.MESH,
            )
    pl.semaphore_wait(barrier, nx + ny + nz - 3)

    ones = jnp.ones((16, columns), bf16)
    sc_z[me_z] = jnp.zeros(sc_z.shape[1:], f32)
    col_all[me_y] = jnp.zeros(col_all.shape[1:], f32)
    for l in range(layers):
        carry = (jnp.zeros((8, columns), f32), jnp.zeros((8, columns), f32))
        for c in range(chunks):
            k = l * chunks + c
            for copy in loads[k]:
                copy.wait()

            def measure(b, carry, k=k):
                col_sum, weight_sum = carry
                block = k * per + b
                here = pl.ds(pl.multiple_of(block * LANES, LANES), LANES)
                grad = g_vm[here, :].astype(f32)
                squares = grad * grad + tiny_term
                row_all[me_z, pl.ds(block, 1), :] = row_dots(ones, squares)[0:1]
                weights = p_vm[here, :]
                return col_sum + fold(squares), weight_sum + fold(weights * weights)

            carry = lax.fori_loop(0, per, measure, carry, unroll=True)
        col_all[me_y, l : l + 1, :] = jnp.sum(carry[0], axis=0, keepdims=True)
        sc_z[me_z, l : l + 1, :] = fold_lanes(jnp.sum(carry[1], axis=0, keepdims=True))
        own = slice(l * nb, (l + 1) * nb)
        row_part = (decay_rate / nz) * row_ref[own, :] + (
            (1.0 - decay_rate) / columns_all
        ) * row_all[me_z, own, :]
        sc_z[me_z, layers + l : layers + l + 1, :] = jnp.sum(row_part, axis=0, keepdims=True)

    first = exchange("gz", (row_all, sc_z), rz_s, rz_r)
    cols = exchange("gy", (col_all,), cy_s, cy_r)
    finish(first)
    sc_y[me_y] = total(sc_z)
    scalars = exchange("gy", (sc_y,), sy_s, sy_r)
    row_new = decay_rate * row_ref[...] + (1.0 - decay_rate) * (total(row_all) / columns_all)
    row_out[...] = row_new
    finish(cols)
    col_new = decay_rate * col_ref[...] + (1.0 - decay_rate) * (
        total(col_all)[0:layers] / rows_all
    )
    col_out[...] = col_new
    finish(scalars)
    sums = jnp.sum(total(sc_y), axis=1, keepdims=True)
    weight_scale = jnp.sqrt(sums[0:layers] / (rows_all * columns_all))
    row_mean = sums[layers : 2 * layers] / rows_all
    for l in range(layers):
        own = slice(l * nb, (l + 1) * nb)
        rr_out[own, :] = lax.rsqrt(row_out[own, :] / row_mean[l : l + 1])
    col_root = lax.rsqrt(col_new)

    lane_sum = jnp.zeros((1, LANES), f32)
    pick = lax.broadcasted_iota(jnp.int32, (16, columns), 0)
    for l in range(layers):
        inverse = jnp.broadcast_to(col_root[l : l + 1] * col_root[l : l + 1], (16, columns))
        top = inverse.astype(bf16).astype(f32)
        mid = (inverse - top).astype(bf16).astype(f32)
        rest = inverse - top - mid
        left = jnp.where(
            pick == 0, top, jnp.where(pick == 1, mid, jnp.where(pick == 2, rest, 0.0))
        ).astype(bf16)

        def weigh(b, acc, first_block, left=left):
            block = first_block + b
            here = pl.ds(pl.multiple_of(block * LANES, LANES), LANES)
            grad = g_vm[here, :].astype(f32)
            sums = jnp.sum(row_dots(left, grad * grad)[0:8], axis=0, keepdims=True)
            root = rr_out[pl.ds(block, 1), :]
            return acc + sums * (root * root)

        def weigh_chunk(c, acc, l=l, weigh=weigh):
            one = functools.partial(weigh, first_block=l * nb + c * per)
            return lax.fori_loop(0, per, one, acc, unroll=True)

        lane_sum = lax.fori_loop(0, chunks, weigh_chunk, lane_sum)

    up_z[me_z] = jnp.broadcast_to(lane_sum, up_z.shape[1:])
    finish(exchange("gz", (up_z,), uz_s, uz_r))
    up_y[me_y] = total(up_z)
    finish(exchange("gy", (up_y,), uy_s, uy_r))
    up_x[me_x] = total(up_y)
    finish(exchange("gx", (up_x,), ux_s, ux_r))
    update_total = jnp.sum(total(up_x)[0:1], axis=1, keepdims=True)
    entries = layers * nx * rows_all * columns_all
    clip_factor = jnp.maximum(1.0, jnp.sqrt(update_total / entries) / clip_limit)
    col_step = col_root * (weight_scale / clip_factor)
    rc_out[...] = col_step

    stores = []
    for l in range(layers):
        for c in range(chunks):
            k = l * chunks + c

            def apply(b, carry, k=k, l=l):
                block = k * per + b
                here = pl.ds(pl.multiple_of(block * LANES, LANES), LANES)
                root = jnp.broadcast_to(rr_out[pl.ds(block, 1), :], (LANES, LANES)).T
                for j in range(0, columns, LANES):
                    cut = slice(j, j + LANES)
                    applied = g_vm[here, cut].astype(f32) * root * col_step[l : l + 1, cut]
                    new_vm[here, cut] = (p_vm[here, cut] - step_share * applied).astype(bf16)
                return carry

            lax.fori_loop(0, per, apply, 0, unroll=True)
            last = k == layers * chunks - 1
            size = chunk - small if last else chunk
            part = pl.ds(k * chunk, size)
            stores.append(pltpu.make_async_copy(new_vm.at[part], big_hbm.at[part], o_sem.at[k]))
            stores[-1].start()
            if last:
                stores.append(
                    pltpu.make_async_copy(
                        new_vm.at[pl.ds(k * chunk + size, small)], small_hbm, o_sem.at[k + 1]
                    )
                )
                stores[-1].start()
    finish(stores)


def statistics(params, grads, row_state, col_state):
    layers, rows, columns = params.shape
    nx, ny, nz = (lax.axis_size(a) for a in ("gx", "gy", "gz"))
    flat = layers * rows
    nb = rows // LANES
    per = max(q for q in range(1, 9) if nb % q == 0)
    chunk = per * LANES
    small = chunk // 2
    count = layers * (rows // chunk)
    tall = -(-2 * layers // 8) * 8
    sem = lambda n: pltpu.SemaphoreType.DMA((max(n, 1),))
    vmem, anywhere = pl.BlockSpec(memory_space=pltpu.VMEM), pl.BlockSpec(memory_space=pl.ANY)
    blocks = flat // LANES
    pairs = [2 * (nz - 1), ny - 1, ny - 1, nz - 1, ny - 1, nx - 1]
    return pl.pallas_call(
        functools.partial(stats_kernel, layers, chunk, small),
        out_shape=(
            jax.ShapeDtypeStruct((blocks, LANES), f32),
            jax.ShapeDtypeStruct((layers, columns), f32),
            jax.ShapeDtypeStruct((blocks, LANES), f32),
            jax.ShapeDtypeStruct((layers, columns), f32),
            jax.ShapeDtypeStruct((flat - small, columns), bf16),
            jax.ShapeDtypeStruct((small, columns), bf16),
        ),
        in_specs=[anywhere, anywhere, vmem, vmem],
        out_specs=(vmem, vmem, vmem, vmem, anywhere, anywhere),
        scratch_shapes=[
            pltpu.VMEM((flat, columns), f32),
            pltpu.VMEM((flat, columns), bf16),
            pltpu.VMEM((flat, columns), bf16),
            pltpu.VMEM((nz, blocks, LANES), f32),
            pltpu.VMEM((ny, -(-layers // 8) * 8, columns), f32),
            pltpu.VMEM((nz, tall, LANES), f32),
            pltpu.VMEM((ny, tall, LANES), f32),
            pltpu.VMEM((nz, 8, LANES), f32),
            pltpu.VMEM((ny, 8, LANES), f32),
            pltpu.VMEM((nx, 8, LANES), f32),
            sem(count),
            sem(count),
            sem(count + 1),
        ]
        + [sem(n) for n in pairs for _ in range(2)],
        compiler_params=pltpu.CompilerParams(
            collective_id=0, has_side_effects=True, vmem_limit_bytes=60 * 1024 * 1024
        ),
        cost_estimate=pl.CostEstimate(
            flops=20 * flat * columns, bytes_accessed=8 * flat * columns, transcendentals=0
        ),
    )(
        params.reshape(flat, columns),
        grads.reshape(flat, columns),
        row_state.reshape(blocks, LANES),
        col_state,
    )


def place_kernel(n, *refs):
    out = refs[-1]
    columns = out.shape[1] // n
    for d in range(n):
        out[:, d * columns : (d + 1) * columns] = refs[d][0]


def place(gathered, held, row0, flat, block):
    n, rows, columns = gathered.shape
    start = row0 // block
    specs = [pl.BlockSpec((1, block, columns), lambda i, d=d: (d, i, 0)) for d in range(n)]
    operands, aliases = [gathered] * n, {}
    if held is not None:
        operands.append(held)
        specs.append(pl.BlockSpec(memory_space=pl.ANY))
        aliases = {n: 0}
    return pl.pallas_call(
        functools.partial(place_kernel, n),
        grid=(rows // block,),
        in_specs=specs,
        out_specs=pl.BlockSpec((block, n * columns), lambda i: (start + i, 0)),
        out_shape=jax.ShapeDtypeStruct((flat, n * columns), bf16),
        input_output_aliases=aliases,
        cost_estimate=pl.CostEstimate(
            flops=0, bytes_accessed=4 * n * rows * columns, transcendentals=0
        ),
    )(*operands)


def body(params, grads, row_state, col_state):
    layers, rows, columns = params.shape
    row_new, col_new, row_root, col_step, big, small = statistics(
        params, grads, row_state, col_state
    )
    big_all = lax.all_gather(big, "gz", axis=0)
    small_all = lax.all_gather(small, "gz", axis=0)
    row_root = row_root.reshape(layers, rows)
    applied = grads.astype(f32) * row_root[:, :, None] * col_step[:, None, :]
    new_params = params - step_share * applied
    flat, block = layers * rows, small.shape[0]
    held = place(big_all, None, 0, flat, block)
    held = place(small_all, held, big.shape[0], flat, block)
    compute = held.reshape(layers, rows, held.shape[1])
    return (new_params, row_new.reshape(layers, rows), col_new, applied, compute)


def solution(mesh):
    in_specs = (P("gx", "gy", "gz"), P("gx", "gy", "gz"), P("gx", "gy"), P("gx", "gz"))
    out_specs = (
        P("gx", "gy", "gz"),
        P("gx", "gy"),
        P("gx", "gz"),
        P("gx", "gy", "gz"),
        P("gx", "gy", None),
    )
    return jax.shard_map(body, mesh=mesh, in_specs=in_specs, out_specs=out_specs, check_vma=False)
```

time: 712 us -> 624 us (0.88)
  blocking collectives: 76.5 us -> 0 us
  Pallas kernels: 0 us -> 75.3 us
  waiting for transfers between devices: 553 us -> 506 us
  other arithmetic: 44.7 us -> 23.7 us
  local copies, waits for them, and re-layouts: 22.9 us -> 4.3 us
    psum x4 -> x0, blocking collectives: 76.5 us -> none  [the longest x1 38.7 us: body(): update_total = lax.psum(jnp.sum(update_sq), ('gx', 'gy', 'gz'))]
    pallas_call x0 -> x3, Pallas kernels: none -> 75.3 us  [the longest x1 42.9 us: statistics(): pl.pallas_call(functools.partial(stats_kernel, layers, chunk, small), out...]
    all_gather x1 -> x2, waiting for transfers between devices: 553 us -> 505 us  [the longest x1 502 us: body(): big_all = lax.all_gather(big, 'gz', axis=0)]
    sub x0 -> x1, other arithmetic: none -> 23.7 us  [body(): new_params = params - step_share * applied]
    convert_element_type x1 -> x0, other arithmetic: 22.5 us -> none  [body(): copy_half = new_params.astype(jnp.bfloat16)]
    unnamed x9 -> x3, local copies, waits for them, and re-layouts: 22.9 us -> 0.6 us
    reduce_sum x4 -> x0, other arithmetic: 22.1 us -> none  [the longest x1 8.24 us: body(): update_total = lax.psum(jnp.sum(update_sq), ('gx', 'gy', 'gz'))]
  transfers between devices with their start and end apart: 1 -> 2, of which waited for: 1 -> 2; matrix products, arithmetic and copies ran while one was open for 0% -> 4% of each run, Pallas kernels for 0% -> 5%
where the time goes in v1:
time: 624 us; the launch traced here: 623 us
  waiting for transfers between devices  506 us (81%)
  Pallas kernels  75.3 us (12%)
  other arithmetic  23.7 us (4%)
  between operations  14.1 us (2%)
    all_gather x1, waiting for transfers between devices, body(): big_all = lax.all_gather(big, 'gz', axis=0)  502 us
    pallas_call x1, Pallas kernels, statistics(): pl.pallas_call(functools.partial(stats_kernel, layers, chunk, small), out...  42.9 us
    pallas_call x2, Pallas kernels, place(): pl.pallas_call(functools.partial(place_kernel, n), grid=(rows // block,),...  32.4 us
    sub x1, other arithmetic, body(): new_params = params - step_share * applied  23.7 us
  transfers between devices with their start and end apart: 2, of which 2 were waited for; matrix products, arithmetic and copies ran while one was open for 4% of the time, Pallas kernels for 5%

profile of v1, /device:TPU:0, one launch (start us, length us, event | category | flops | bytes accessed | tf_op | source)
XLA Modules:
  0.0 623.4 jit_solution(16942841512558169879)
XLA Ops:
  7.2 0.0 all-gather.7.cloned.1.call-start
  7.2 1.5 reshape.29.row_ref
  8.7 42.9 %shard_map.83 = (f32[84,128]{1,0:T(8,128)}, f32[3,384]{1,0:T(4,128)}, f32[84,128]{1,0:T(8,128)}, f32[3,384]{1,0:T(4,128)}, bf16[10304,384]{1,0:T(8,128)(2,1)}, /*index=5*/bf16[448,384]{1,0:T(8,128)(2,1)}) custom-call(f32[10752,384]{1,0:T(8,128)} %bitcast.10, bf16[10752,384]{1,0:T(8,128)(2,1)} %bitcast.11, f32[84,128]{1,0:T(8,128)} %reshape.29.row_ref, ...), custom_call_target="tpu_custom_call" | custom-call | flops 82575360 | bytes 33030144 | tf_op jit(solution)/shard_map/pallas_call | solution.py:231
  51.6 0.0 all-gather.7.cloned.1.call-update
  51.6 0.0 all-gather.5.cloned.1.call-start
  51.7 0.7 all-gather.5.cloned.1.call-update
  52.4 0.8 mul.24
  53.2 1.4 reshape.30
  54.6 23.7 %multiply_subtract_fusion = (f32[3,3584,384]{2,1,0:T(8,128)}, f32[3,3584,384]{2,1,0:T(8,128)}) fusion(f32[3,3584,384]{2,1,0:T(8,128)} %param.4, f32[3,384]{1,0:T(4,128)} %get-tuple-element.12, f32[3,3584]{1,0:T(4,128)S(1)} %mul.24, bf16[3,3584,384]{2,1,0:T(8,128)(2,1)} %param.5), kind=kLoop, calls=%fused_computation | loop fusion | flops 20643840 | bytes 57850368 | tf_op jit(solution)/shard_map/sub | solution.py:311
  78.4 501.6 %all-gather.7.cloned.1.call-done = bf16[41216,384]{1,0:T(8,128)(2,1)} async-done(((bf16[10304,384]{1,0:T(8,128)(2,1)}), bf16[41216,384]{1,0:T(8,128)(2,1)}) %all-gather.7.cloned.1.call-update) | async-done | bytes 31653904 | tf_op jit(solution)/shard_map/all_gather | solution.py:307
  580.0 29.9 %shard_map.84.refs_4_ = bf16[10752,1536]{1,0:T(8,128)(2,1)} custom-call(bf16[4,10304,384]{2,1,0:T(8,128)(2,1)} %bitcast.5, bf16[4,10304,384]{2,1,0:T(8,128)(2,1)} %bitcast.6, bf16[4,10304,384]{2,1,0:T(8,128)(2,1)} %bitcast.7, bf16[4,10304,384]{2,1,0:T(8,128)(2,1)} %bitcast.8), custom_call_target="tpu_custom_call" | custom-call | bytes 63307776 | tf_op jit(solution)/shard_map/pallas_call | solution.py:289
  609.9 3.5 all-gather.5.cloned.1.call-done
  613.4 0.0 copy-start
  613.4 2.5 shard_map.85
  615.9 0.0 copy-done
  615.9 0.6 copy.12
Async XLA Ops:
  7.2 572.8 %all-gather.7.cloned.1.call-start = ((), (), s32[]{:S(2)}) async-start(), calls=%async_computation.1 | async-start | bytes 39567360 | tf_op jit(solution)/shard_map/all_gather | solution.py:307
  51.6 561.8 %all-gather.5.cloned.1.call-start = ((), (), s32[]{:S(2)}) async-start(), calls=%async_computation | async-start | bytes 1720320 | tf_op jit(solution)/shard_map/all_gather | solution.py:308
  613.4 2.5 copy-start
Sparse Core Ops, SparseCore 0:
  51.8 528.2 all-gather.6
  581.6 31.8 all-gather.4
